TPU v7x, 32 devices: a whole 2x2x4 slice. The times are simulated.
32 devices in a mesh: tm: 4 (over y, core), space: 8 (over z, x).
Axes of the slice: x: 2, y: 2, z: 4, core: 2. Of those that a mesh axis runs over, the one named last changes fastest.
Arguments:
- perm_field: float32 [4, 32, 32, 256], P(None, 'space'), may hold values from 0.5 to 2
- step_multiplier: float32 [4, 32, 32, 256], P('tm', 'space'), may hold values from 0.5 to 2
- inflow: float32 [4, 32, 32, 256], P('tm', 'space'), may hold values from -3 to 3
- start_pressure: float32 [32, 32, 256], P('space'), may hold values from -6 to 6
- start_saturation: float32 [32, 32, 256], P('space'), may hold values from 0.1 to 0.9
- region_ids: int32 [32, 32, 256], P('space'), may hold values from 0 to 7
- region_table: float32 [3, 8], replicated, may hold values from 0.25 to 2
- well_cells: int32 [32], replicated, may hold values from 0 to 262143
- well_rates: float32 [4, 32], P('tm'), may hold values from -8 to 8
- observed: float32 [4, 4, 32], P(None, 'tm'), may hold values from -6 to 6
Outputs:
- misfit: float32 [4], replicated
- slab_pressure: float32 [4, 4, 32, 32, 256], P('tm', None, 'space')
- slab_saturation: float32 [4, 4, 32, 32, 256], P('tm', None, 'space')
All inputs are finite; a program needn't handle non-finite values.
Results may differ from a plain program's by a relative error of at most 0.0003.
Values sent between devices are 32-bit elements; how exact they have to be, the bound alone decides.
A program may use at most 64 MiB of HBM per device.

v0:
```python
import jax
import jax.numpy as jnp
from jax import lax
from jax.sharding import PartitionSpec as P

MB = 1
REP_DEV = 1
ITERS = 3


def padded(cells, sides, width):
    for axis, dim in sides:
        count = lax.axis_size(axis)
        ends = count - 1
        head = lax.slice_in_dim(cells, 0, width, axis=dim)
        tail = lax.slice_in_dim(cells, cells.shape[dim] - width, cells.shape[dim], axis=dim)
        cells = jnp.concatenate(
            [
                lax.ppermute(tail, axis, [(i, (i + 1) % count) for i in range(ends)]),
                cells,
                lax.ppermute(head, axis, [((i + 1) % count, i) for i in range(ends)]),
            ],
            axis=dim,
        )
    return cells


def shifted(values, dimension, offset):
    margins = [(0, 0)] * values.ndim
    length = values.shape[dimension]
    if offset > 0:
        margins[dimension] = (1, 0)
        return lax.slice_in_dim(jnp.pad(values, margins), 0, length, axis=dimension)
    margins[dimension] = (0, 1)
    return lax.slice_in_dim(jnp.pad(values, margins), 1, length + 1, axis=dimension)


def neighbour_values(values_ext):
    middle = values_ext[:, 1:-1]
    return (
        values_ext[:, :-2],
        values_ext[:, 2:],
        shifted(middle, 2, 1),
        shifted(middle, 2, -1),
        shifted(middle, 3, 1),
        shifted(middle, 3, -1),
    )


def coefficients(conduct_ext):
    middle = conduct_ext[:, 1:-1]
    others = neighbour_values(conduct_ext)
    links = [jnp.sqrt(middle * other_side) for other_side in others]
    link_total = links[0] + links[1] + links[2] + links[3] + links[4] + links[5]
    return tuple(links) + (link_total,)


def jacobi_sweep(pressure_ext, couplings, storage, right_side):
    beside = neighbour_values(pressure_ext)
    inflowing = couplings[0] * beside[0]
    for link_index in range(1, 6):
        inflowing = inflowing + couplings[link_index] * beside[link_index]
    divisor = jnp.where(storage > 0, storage + couplings[6], 1.0)
    return (right_side + inflowing) / divisor


def fraction(saturation, ratio):
    squared = saturation * saturation
    remain = (1.0 - saturation) * (1.0 - saturation)
    return squared / (squared + ratio * remain)


def transport(pressure_ext, flow_ext, couplings, saturation, gain, source):
    centre_p = pressure_ext[:, 1:-1]
    centre_f = flow_ext[:, 1:-1]
    other_p = neighbour_values(pressure_ext)
    other_f = neighbour_values(flow_ext)
    outflow = None
    for link_index in range(6):
        face_flux = couplings[link_index] * (centre_p - other_p[link_index])
        carried = face_flux * jnp.where(face_flux > 0, centre_f, other_f[link_index])
        outflow = carried if outflow is None else outflow + carried
    gained = (
        jnp.maximum(source, 0.0) * (1.0 - saturation)
        - jnp.maximum(-source, 0.0) * centre_f
        - outflow
    )
    return saturation + gain * gained


def region_fields(region_ids, region_table):
    fields = []
    for table_row in range(3):
        summed = jnp.zeros(region_ids.shape, jnp.float32)
        for region_index in range(region_table.shape[1]):
            summed = summed + jnp.where(
                region_ids == region_index, region_table[table_row, region_index], 0.0
            )
        fields.append(summed)
    return (fields[0], fields[1], 0.1 * fields[2])


def advance(pressure, saturation, conduct, source, inflow_now, storage, ratio, gain):
    right_side = storage * pressure + source + inflow_now
    flow_frac = fraction(saturation, ratio)
    edges = padded(jnp.stack([conduct, pressure]), (("space", 2),), 1)
    couplings = coefficients(edges[0])
    iterate_ext = edges[1]
    iterate = pressure
    for sweep_index in range(ITERS):
        if sweep_index > 0:
            iterate_ext = padded(iterate, (("space", 1),), 1)
        iterate = jacobi_sweep(iterate_ext, couplings, storage, right_side)
    both = padded(jnp.stack([iterate, flow_frac]), (("space", 2),), 1)
    saturation = transport(both[0], both[1], couplings, saturation, gain, source)
    return (iterate, saturation)


def body(
    perm_field,
    step_multiplier,
    inflow,
    start_pressure,
    start_saturation,
    region_ids,
    region_table,
    well_cells,
    well_rates,
    observed,
):
    sections = lax.axis_size("tm")
    section_index = lax.axis_index("tm")
    space_index = lax.axis_index("space")
    grid_shape = start_pressure.shape
    width_x, depth, across = grid_shape
    batch_size = MB
    storage, ratio, gain = region_fields(region_ids, region_table)
    layer_ids = lax.broadcasted_iota(jnp.int32, grid_shape, 0) + space_index * width_x
    cell_ids = (
        layer_ids * depth + lax.broadcasted_iota(jnp.int32, grid_shape, 1)
    ) * across + lax.broadcasted_iota(jnp.int32, grid_shape, 2)
    well_picks = (well_cells[:, None] == cell_ids.reshape(1, -1)).astype(jnp.float32)
    well_owned = jnp.sum(well_picks, axis=1)
    start_p = jnp.broadcast_to(start_pressure, (batch_size,) + grid_shape)
    start_s = jnp.broadcast_to(start_saturation, (batch_size,) + grid_shape)

    def mismatch(pressure, measured):
        predicted = jnp.dot(
            pressure.reshape(batch_size, -1), well_picks.T, precision=lax.Precision.HIGHEST
        )
        return jnp.sum(well_owned * (predicted - measured) ** 2, axis=1)

    misfit = jnp.zeros((perm_field.shape[0],), jnp.float32)
    fields = (
        lax.all_gather(step_multiplier, "tm", axis=0, tiled=True),
        lax.all_gather(inflow, "tm", axis=0, tiled=True),
        lax.all_gather(well_rates, "tm", axis=0, tiled=True),
    )
    measured_all = lax.all_to_all(observed, "tm", split_axis=0, concat_axis=1, tiled=True)
    perm_rows = lax.dynamic_slice_in_dim(perm_field, section_index * batch_size, batch_size, 0)
    rate_rows = fields[2]
    placed = jnp.dot(rate_rows, well_picks, precision=lax.Precision.HIGHEST)
    all_sources = placed.reshape((rate_rows.shape[0],) + grid_shape)
    zero_ends = jnp.zeros((sections, batch_size) + grid_shape, jnp.float32)

    def one_section(slab_index, state_tuple):
        pressure, saturation, ends_p, ends_s, errors = state_tuple
        position = slab_index * REP_DEV + 0
        multiplier = lax.dynamic_index_in_dim(fields[0], position, 0, keepdims=False)
        inflow_now = lax.dynamic_index_in_dim(fields[1], position, 0, keepdims=False)
        source = lax.dynamic_index_in_dim(all_sources, position, 0, keepdims=False)
        pressure, saturation = advance(
            pressure, saturation, perm_rows * multiplier, source, inflow_now, storage, ratio, gain
        )
        errors = errors + mismatch(
            pressure, lax.dynamic_index_in_dim(measured_all, position, 1, keepdims=False)
        )
        ends_p = lax.dynamic_update_index_in_dim(ends_p, pressure, slab_index, 0)
        ends_s = lax.dynamic_update_index_in_dim(ends_s, saturation, slab_index, 0)
        return (pressure, saturation, ends_p, ends_s, errors)

    result = lax.fori_loop(
        0,
        sections,
        one_section,
        (start_p, start_s, zero_ends, zero_ends, jnp.zeros((batch_size,), jnp.float32)),
    )
    slab_pressure, slab_saturation = (
        lax.all_to_all(result[2], "tm", split_axis=0, concat_axis=1, tiled=True),
        lax.all_to_all(result[3], "tm", split_axis=0, concat_axis=1, tiled=True),
    )
    misfit = lax.dynamic_update_slice_in_dim(misfit, result[4], section_index * batch_size, 0)
    totals = lax.psum(misfit, ("tm", "space"))
    return (totals / (sections * REP_DEV * well_cells.shape[0]), slab_pressure, slab_saturation)


def solution(mesh):
    return jax.shard_map(
        body,
        mesh=mesh,
        in_specs=(
            P(None, "space", None, None),
            P("tm", "space", None, None),
            P("tm", "space", None, None),
            P("space", None, None),
            P("space", None, None),
            P("space", None, None),
            P(),
            P(),
            P("tm", None),
            P(None, "tm", None),
        ),
        out_specs=(P(), P("tm", None, "space", None, None), P("tm", None, "space", None, None)),
        check_vma=False,
    )
```

profile of v0, /device:TPU:0, one launch (start us, length us, event | category | flops | bytes accessed | tf_op | source)
XLA Modules:
  0.0 281.1 jit_solution(10147886916045654952)
XLA Ops:
  6.7 5.2 %all-gather = f32[4,1,32]{2,1,0:T(1,128)S(1)} all-gather(f32[1,1,32]{2,1,0:T(1,128)S(1)} %bitcast.154), channel_id=1, replica_groups=mesh['tm'=4,'space'=8] {'tm'}, dimensions={0}, use_global_device_ids=true | all-gather | bytes 640 | tf_op jit(solution)/shard_map/all_gather | solution.py:157
  13.9 8.2 %all_gather.10 = f32[4,4,32,256]{3,2,1,0:T(8,128)} all-gather(f32[1,4,32,256]{3,2,1,0:T(8,128)S(1)} %copy-done.7), channel_id=1, replica_groups=mesh['tm'=4,'space'=8] {'tm'}, dimensions={0}, use_global_device_ids=true | all-gather | bytes 655360 | tf_op jit(solution)/shard_map/all_gather | solution.py:156
  22.1 7.4 %all_gather.11 = f32[4,4,32,256]{3,2,1,0:T(8,128)S(1)} all-gather(f32[1,4,32,256]{3,2,1,0:T(8,128)S(1)} %copy-done.8), channel_id=1, replica_groups=mesh['tm'=4,'space'=8] {'tm'}, dimensions={0}, use_global_device_ids=true | all-gather | bytes 655360 | tf_op jit(solution)/shard_map/all_gather | solution.py:155
  29.6 5.2 %select_add_fusion = (f32[4,32,256]{2,1,0:T(8,128)S(1)}, pred[4,32,256]{2,1,0:T(8,128)(4,1)S(1)}, pred[4,32,256]{2,1,0:T(8,128)(4,1)S(1)}, pred[4,32,256]{2,1,0:...) fusion(f32[]{:T(128)} %bitcast.28, f32[]{:T(128)} %bitcast.27, ...), kind=kLoop, calls=%fused_computation.152 | loop fusion | flops 753664 | bytes 524320 | tf_op jit(solution)/shard_map/add | solution.py:96
  34.8 5.1 %add_multiply_fusion = f32[4,32,256]{2,1,0:T(8,128)S(1)} fusion(pred[4,32,256]{2,1,0:T(8,128)(4,1)S(1)} %get-tuple-element.474, pred[4,32,256]{2,1,0:T(8,128)(4,1)S(1)} %get-tuple-element.473, pred[4,32,256]{2,1,0:T(8,128)(4,1)S(1)} %get-tuple-element.472, pred[4,32,256]{2,1,0:T(8,128)(4,1)S(1)} %get-tuple-element.471, ...), kind=kLoop, calls=%fused_computation.153 | loop fusion | flops 524288 | bytes 393248 | tf_op jit(solution)/shard_map/mul | solution.py:100
  39.8 5.1 %select_add_fusion.1 = f32[4,32,256]{2,1,0:T(8,128)S(1)} fusion(pred[4,32,256]{2,1,0:T(8,128)(4,1)S(1)} %get-tuple-element.474, pred[4,32,256]{2,1,0:T(8,128)(4,1)S(1)} %get-tuple-element.473, pred[4,32,256]{2,1,0:T(8,128)(4,1)S(1)} %get-tuple-element.472, pred[4,32,256]{2,1,0:T(8,128)(4,1)S(1)} %get-tuple-element.471, ...), kind=kLoop, calls=%fused_computation.155 | loop fusion | flops 491520 | bytes 393248 | tf_op jit(solution)/shard_map/add | solution.py:96
  46.0 170.8 %while.24 = (s32[]{:T(128)}, f32[1,4,32,256]{3,2,1,0:T(8,128)S(1)}, f32[1,4,32,256]{3,2,1,0:T(8,128)S(1)}, f32[4,1,4,32,256]{4,3,2,1,0:T(8,128)}, f32[4,1,4,32,2...) while((s32[]{:T(128)}, f32[1,4,32,256]{3,2,1,0:T(8,128)S(1)}, ...), condition=%wide.region_3.4_spmd.clone, body=%wide.region_1.3_spmd.clone.sunk | while | flops 19529856 | bytes 16516069 | solution.py:182
  56.7 5.1 %collective-permute-start.3 = (f32[1,1,32,256]{3,2,1,0:T(8,128)S(1)}, f32[1,1,32,256]{3,2,1,0:T(8,128)S(1)}, u32[]{:S(2)}, u32[]{:S(2)}) collective-permute-start(f32[1,1,32,256]{3,2,1,0:T(8,128)S(1)} %get-tuple-element.656), channel_id=1, source_target_pairs={{0,1},{1,2},{2,3},{3,4},{4,5},{5,6},{6,7},{8,9},{9,10},{10,11},{11... | collective-permute-start | bytes 98312 | tf_op jit(solution)/shard_map/while/body/eval_jaxpr/ppermute | solution.py:19
  64.9 5.8 %collective-permute-start.5 = (f32[1,1,32,256]{3,2,1,0:T(8,128)S(1)}, f32[1,1,32,256]{3,2,1,0:T(8,128)S(1)}, u32[]{:S(2)}, u32[]{:S(2)}) collective-permute-start(f32[1,1,32,256]{3,2,1,0:T(8,128)S(1)} %get-tuple-element.658), channel_id=1, source_target_pairs={{0,1},{1,2},{2,3},{3,4},{4,5},{5,6},{6,7},{8,9},{9,10},{10,11},{11... | collective-permute-start | bytes 98312 | tf_op jit(solution)/shard_map/while/body/eval_jaxpr/ppermute | solution.py:19
  75.9 5.8 %collective-permute-start.7 = (f32[2,1,1,32,256]{4,3,2,1,0:T(8,128)S(1)}, f32[2,1,1,32,256]{4,3,2,1,0:T(8,128)S(1)}, u32[]{:S(2)}, u32[]{:S(2)}) collective-permute-start(f32[2,1,1,32,256]{4,3,2,1,0:T(8,128)S(1)} %get-tuple-element.662), channel_id=1, source_target_pairs={{0,1},{1,2},{2,3},{3,4},{4,5},{5,6},{6,7},{8,9},{9,10},{10,11},{11... | collective-permute-start | bytes 196616 | tf_op jit(solution)/shard_map/while/body/eval_jaxpr/ppermute | solution.py:19
  88.9 5.8 %collective-permute-start.1 = (f32[2,1,1,32,256]{4,3,2,1,0:T(8,128)S(1)}, f32[2,1,1,32,256]{4,3,2,1,0:T(8,128)S(1)}, u32[]{:S(2)}, u32[]{:S(2)}) collective-permute-start(f32[2,1,1,32,256]{4,3,2,1,0:T(8,128)S(1)} %get-tuple-element.644), channel_id=1, source_target_pairs={{0,1},{1,2},{2,3},{3,4},{4,5},{5,6},{6,7},{8,9},{9,10},{10,11},{11... | collective-permute-start | bytes 196616 | tf_op jit(solution)/shard_map/while/body/eval_jaxpr/ppermute | solution.py:19
  99.3 5.4 %collective-permute-start.3 = (f32[1,1,32,256]{3,2,1,0:T(8,128)S(1)}, f32[1,1,32,256]{3,2,1,0:T(8,128)S(1)}, u32[]{:S(2)}, u32[]{:S(2)}) collective-permute-start(f32[1,1,32,256]{3,2,1,0:T(8,128)S(1)} %get-tuple-element.656), channel_id=1, source_target_pairs={{0,1},{1,2},{2,3},{3,4},{4,5},{5,6},{6,7},{8,9},{9,10},{10,11},{11... | collective-permute-start | bytes 98312 | tf_op jit(solution)/shard_map/while/body/eval_jaxpr/ppermute | solution.py:19
  107.8 5.8 %collective-permute-start.5 = (f32[1,1,32,256]{3,2,1,0:T(8,128)S(1)}, f32[1,1,32,256]{3,2,1,0:T(8,128)S(1)}, u32[]{:S(2)}, u32[]{:S(2)}) collective-permute-start(f32[1,1,32,256]{3,2,1,0:T(8,128)S(1)} %get-tuple-element.658), channel_id=1, source_target_pairs={{0,1},{1,2},{2,3},{3,4},{4,5},{5,6},{6,7},{8,9},{9,10},{10,11},{11... | collective-permute-start | bytes 98312 | tf_op jit(solution)/shard_map/while/body/eval_jaxpr/ppermute | solution.py:19
  118.8 5.8 %collective-permute-start.7 = (f32[2,1,1,32,256]{4,3,2,1,0:T(8,128)S(1)}, f32[2,1,1,32,256]{4,3,2,1,0:T(8,128)S(1)}, u32[]{:S(2)}, u32[]{:S(2)}) collective-permute-start(f32[2,1,1,32,256]{4,3,2,1,0:T(8,128)S(1)} %get-tuple-element.662), channel_id=1, source_target_pairs={{0,1},{1,2},{2,3},{3,4},{4,5},{5,6},{6,7},{8,9},{9,10},{10,11},{11... | collective-permute-start | bytes 196616 | tf_op jit(solution)/shard_map/while/body/eval_jaxpr/ppermute | solution.py:19
  131.8 5.9 %collective-permute-start.1 = (f32[2,1,1,32,256]{4,3,2,1,0:T(8,128)S(1)}, f32[2,1,1,32,256]{4,3,2,1,0:T(8,128)S(1)}, u32[]{:S(2)}, u32[]{:S(2)}) collective-permute-start(f32[2,1,1,32,256]{4,3,2,1,0:T(8,128)S(1)} %get-tuple-element.644), channel_id=1, source_target_pairs={{0,1},{1,2},{2,3},{3,4},{4,5},{5,6},{6,7},{8,9},{9,10},{10,11},{11... | collective-permute-start | bytes 196616 | tf_op jit(solution)/shard_map/while/body/eval_jaxpr/ppermute | solution.py:19
  142.6 5.4 %collective-permute-start.3 = (f32[1,1,32,256]{3,2,1,0:T(8,128)S(1)}, f32[1,1,32,256]{3,2,1,0:T(8,128)S(1)}, u32[]{:S(2)}, u32[]{:S(2)}) collective-permute-start(f32[1,1,32,256]{3,2,1,0:T(8,128)S(1)} %get-tuple-element.656), channel_id=1, source_target_pairs={{0,1},{1,2},{2,3},{3,4},{4,5},{5,6},{6,7},{8,9},{9,10},{10,11},{11... | collective-permute-start | bytes 98312 | tf_op jit(solution)/shard_map/while/body/eval_jaxpr/ppermute | solution.py:19
  151.0 5.9 %collective-permute-start.5 = (f32[1,1,32,256]{3,2,1,0:T(8,128)S(1)}, f32[1,1,32,256]{3,2,1,0:T(8,128)S(1)}, u32[]{:S(2)}, u32[]{:S(2)}) collective-permute-start(f32[1,1,32,256]{3,2,1,0:T(8,128)S(1)} %get-tuple-element.658), channel_id=1, source_target_pairs={{0,1},{1,2},{2,3},{3,4},{4,5},{5,6},{6,7},{8,9},{9,10},{10,11},{11... | collective-permute-start | bytes 98312 | tf_op jit(solution)/shard_map/while/body/eval_jaxpr/ppermute | solution.py:19
  162.2 5.7 %collective-permute-start.7 = (f32[2,1,1,32,256]{4,3,2,1,0:T(8,128)S(1)}, f32[2,1,1,32,256]{4,3,2,1,0:T(8,128)S(1)}, u32[]{:S(2)}, u32[]{:S(2)}) collective-permute-start(f32[2,1,1,32,256]{4,3,2,1,0:T(8,128)S(1)} %get-tuple-element.662), channel_id=1, source_target_pairs={{0,1},{1,2},{2,3},{3,4},{4,5},{5,6},{6,7},{8,9},{9,10},{10,11},{11... | collective-permute-start | bytes 196616 | tf_op jit(solution)/shard_map/while/body/eval_jaxpr/ppermute | solution.py:19
  175.2 5.8 %collective-permute-start.1 = (f32[2,1,1,32,256]{4,3,2,1,0:T(8,128)S(1)}, f32[2,1,1,32,256]{4,3,2,1,0:T(8,128)S(1)}, u32[]{:S(2)}, u32[]{:S(2)}) collective-permute-start(f32[2,1,1,32,256]{4,3,2,1,0:T(8,128)S(1)} %get-tuple-element.644), channel_id=1, source_target_pairs={{0,1},{1,2},{2,3},{3,4},{4,5},{5,6},{6,7},{8,9},{9,10},{10,11},{11... | collective-permute-start | bytes 196616 | tf_op jit(solution)/shard_map/while/body/eval_jaxpr/ppermute | solution.py:19
  185.6 5.4 %collective-permute-start.3 = (f32[1,1,32,256]{3,2,1,0:T(8,128)S(1)}, f32[1,1,32,256]{3,2,1,0:T(8,128)S(1)}, u32[]{:S(2)}, u32[]{:S(2)}) collective-permute-start(f32[1,1,32,256]{3,2,1,0:T(8,128)S(1)} %get-tuple-element.656), channel_id=1, source_target_pairs={{0,1},{1,2},{2,3},{3,4},{4,5},{5,6},{6,7},{8,9},{9,10},{10,11},{11... | collective-permute-start | bytes 98312 | tf_op jit(solution)/shard_map/while/body/eval_jaxpr/ppermute | solution.py:19
  194.1 5.8 %collective-permute-start.5 = (f32[1,1,32,256]{3,2,1,0:T(8,128)S(1)}, f32[1,1,32,256]{3,2,1,0:T(8,128)S(1)}, u32[]{:S(2)}, u32[]{:S(2)}) collective-permute-start(f32[1,1,32,256]{3,2,1,0:T(8,128)S(1)} %get-tuple-element.658), channel_id=1, source_target_pairs={{0,1},{1,2},{2,3},{3,4},{4,5},{5,6},{6,7},{8,9},{9,10},{10,11},{11... | collective-permute-start | bytes 98312 | tf_op jit(solution)/shard_map/while/body/eval_jaxpr/ppermute | solution.py:19
  205.1 5.8 %collective-permute-start.7 = (f32[2,1,1,32,256]{4,3,2,1,0:T(8,128)S(1)}, f32[2,1,1,32,256]{4,3,2,1,0:T(8,128)S(1)}, u32[]{:S(2)}, u32[]{:S(2)}) collective-permute-start(f32[2,1,1,32,256]{4,3,2,1,0:T(8,128)S(1)} %get-tuple-element.662), channel_id=1, source_target_pairs={{0,1},{1,2},{2,3},{3,4},{4,5},{5,6},{6,7},{8,9},{9,10},{10,11},{11... | collective-permute-start | bytes 196616 | tf_op jit(solution)/shard_map/while/body/eval_jaxpr/ppermute | solution.py:19
  216.8 12.3 %all_to_all.36 = f32[4,1,4,32,256]{4,3,2,1,0:T(8,128)S(1)} all-to-all(f32[4,1,4,32,256]{4,3,2,1,0:T(8,128)} %get-tuple-element.380), channel_id=1, replica_groups=mesh['tm'=4,'space'=8] {'tm'}, dimensions={0} | all-to-all | bytes 1048576 | tf_op jit(solution)/shard_map/all_to_all | solution.py:189
  232.6 46.4 %psum.7 = f32[4]{0:T(128)S(1)} all-reduce(f32[4]{0:T(128)S(1)} %dynamic_update_slice.24), channel_id=1, replica_groups=mesh['tm'=4,'space'=8] {'tm','space'}, use_global_device_ids=true, to_apply=%region_4.5 | all-reduce | flops 4 | bytes 32 | tf_op jit(solution)/shard_map/psum | solution.py:193
  (189 shorter events, 97.1 us)
Async XLA Ops:
  0.7 44.4 %all-to-all-start = ((f32[4,1,32]{2,1,0:T(1,128)}), f32[4,1,32]{2,1,0:T(1,128)S(1)}, u32[]{:S(2)}, u32[]{:S(2)}) async-start(f32[4,1,32]{2,1,0:T(1,128)} %param.21), calls=%async_computation | async-start | bytes 4096 | tf_op jit(solution)/shard_map/all_to_all | solution.py:159
  63.6 7.1 %collective-permute-start.4 = (f32[1,1,32,256]{3,2,1,0:T(8,128)S(1)}, f32[1,1,32,256]{3,2,1,0:T(8,128)S(1)}, u32[]{:S(2)}, u32[]{:S(2)}) collective-permute-start(f32[1,1,32,256]{3,2,1,0:T(8,128)S(1)} %get-tuple-element.657), channel_id=1, source_target_pairs={{1,0},{2,1},{3,2},{4,3},{5,4},{6,5},{7,6},{9,8},{10,9},{11,10},{12... | collective-permute-start | bytes 98312 | tf_op jit(solution)/shard_map/while/body/eval_jaxpr/ppermute | solution.py:21
  64.9 7.4 %collective-permute-start.5 = (f32[1,1,32,256]{3,2,1,0:T(8,128)S(1)}, f32[1,1,32,256]{3,2,1,0:T(8,128)S(1)}, u32[]{:S(2)}, u32[]{:S(2)}) collective-permute-start(f32[1,1,32,256]{3,2,1,0:T(8,128)S(1)} %get-tuple-element.658), channel_id=1, source_target_pairs={{0,1},{1,2},{2,3},{3,4},{4,5},{5,6},{6,7},{8,9},{9,10},{10,11},{11... | collective-permute-start | bytes 98312 | tf_op jit(solution)/shard_map/while/body/eval_jaxpr/ppermute | solution.py:19
  74.4 12.0 %collective-permute-start.6 = (f32[2,1,1,32,256]{4,3,2,1,0:T(8,128)S(1)}, f32[2,1,1,32,256]{4,3,2,1,0:T(8,128)S(1)}, u32[]{:S(2)}, u32[]{:S(2)}) collective-permute-start(f32[2,1,1,32,256]{4,3,2,1,0:T(8,128)S(1)} %get-tuple-element.661), channel_id=1, source_target_pairs={{1,0},{2,1},{3,2},{4,3},{5,4},{6,5},{7,6},{9,8},{10,9},{11,10},{12... | collective-permute-start | bytes 196616 | tf_op jit(solution)/shard_map/while/body/eval_jaxpr/ppermute | solution.py:21
  75.9 10.6 %collective-permute-start.7 = (f32[2,1,1,32,256]{4,3,2,1,0:T(8,128)S(1)}, f32[2,1,1,32,256]{4,3,2,1,0:T(8,128)S(1)}, u32[]{:S(2)}, u32[]{:S(2)}) collective-permute-start(f32[2,1,1,32,256]{4,3,2,1,0:T(8,128)S(1)} %get-tuple-element.662), channel_id=1, source_target_pairs={{0,1},{1,2},{2,3},{3,4},{4,5},{5,6},{6,7},{8,9},{9,10},{10,11},{11... | collective-permute-start | bytes 196616 | tf_op jit(solution)/shard_map/while/body/eval_jaxpr/ppermute | solution.py:19
  87.6 7.4 %collective-permute-start = (f32[2,1,1,32,256]{4,3,2,1,0:T(8,128)S(1)}, f32[2,1,1,32,256]{4,3,2,1,0:T(8,128)S(1)}, u32[]{:S(2)}, u32[]{:S(2)}) collective-permute-start(f32[2,1,1,32,256]{4,3,2,1,0:T(8,128)S(1)} %get-tuple-element.643), channel_id=1, source_target_pairs={{1,0},{2,1},{3,2},{4,3},{5,4},{6,5},{7,6},{9,8},{10,9},{11,10},{12... | collective-permute-start | bytes 196616 | tf_op jit(solution)/shard_map/while/body/eval_jaxpr/ppermute | solution.py:21
  88.9 7.6 %collective-permute-start.1 = (f32[2,1,1,32,256]{4,3,2,1,0:T(8,128)S(1)}, f32[2,1,1,32,256]{4,3,2,1,0:T(8,128)S(1)}, u32[]{:S(2)}, u32[]{:S(2)}) collective-permute-start(f32[2,1,1,32,256]{4,3,2,1,0:T(8,128)S(1)} %get-tuple-element.644), channel_id=1, source_target_pairs={{0,1},{1,2},{2,3},{3,4},{4,5},{5,6},{6,7},{8,9},{9,10},{10,11},{11... | collective-permute-start | bytes 196616 | tf_op jit(solution)/shard_map/while/body/eval_jaxpr/ppermute | solution.py:19
  106.5 7.1 %collective-permute-start.4 = (f32[1,1,32,256]{3,2,1,0:T(8,128)S(1)}, f32[1,1,32,256]{3,2,1,0:T(8,128)S(1)}, u32[]{:S(2)}, u32[]{:S(2)}) collective-permute-start(f32[1,1,32,256]{3,2,1,0:T(8,128)S(1)} %get-tuple-element.657), channel_id=1, source_target_pairs={{1,0},{2,1},{3,2},{4,3},{5,4},{6,5},{7,6},{9,8},{10,9},{11,10},{12... | collective-permute-start | bytes 98312 | tf_op jit(solution)/shard_map/while/body/eval_jaxpr/ppermute | solution.py:21
  107.8 7.4 %collective-permute-start.5 = (f32[1,1,32,256]{3,2,1,0:T(8,128)S(1)}, f32[1,1,32,256]{3,2,1,0:T(8,128)S(1)}, u32[]{:S(2)}, u32[]{:S(2)}) collective-permute-start(f32[1,1,32,256]{3,2,1,0:T(8,128)S(1)} %get-tuple-element.658), channel_id=1, source_target_pairs={{0,1},{1,2},{2,3},{3,4},{4,5},{5,6},{6,7},{8,9},{9,10},{10,11},{11... | collective-permute-start | bytes 98312 | tf_op jit(solution)/shard_map/while/body/eval_jaxpr/ppermute | solution.py:19
  117.4 12.0 %collective-permute-start.6 = (f32[2,1,1,32,256]{4,3,2,1,0:T(8,128)S(1)}, f32[2,1,1,32,256]{4,3,2,1,0:T(8,128)S(1)}, u32[]{:S(2)}, u32[]{:S(2)}) collective-permute-start(f32[2,1,1,32,256]{4,3,2,1,0:T(8,128)S(1)} %get-tuple-element.661), channel_id=1, source_target_pairs={{1,0},{2,1},{3,2},{4,3},{5,4},{6,5},{7,6},{9,8},{10,9},{11,10},{12... | collective-permute-start | bytes 196616 | tf_op jit(solution)/shard_map/while/body/eval_jaxpr/ppermute | solution.py:21
  118.8 10.6 %collective-permute-start.7 = (f32[2,1,1,32,256]{4,3,2,1,0:T(8,128)S(1)}, f32[2,1,1,32,256]{4,3,2,1,0:T(8,128)S(1)}, u32[]{:S(2)}, u32[]{:S(2)}) collective-permute-start(f32[2,1,1,32,256]{4,3,2,1,0:T(8,128)S(1)} %get-tuple-element.662), channel_id=1, source_target_pairs={{0,1},{1,2},{2,3},{3,4},{4,5},{5,6},{6,7},{8,9},{9,10},{10,11},{11... | collective-permute-start | bytes 196616 | tf_op jit(solution)/shard_map/while/body/eval_jaxpr/ppermute | solution.py:19
  130.5 7.6 %collective-permute-start = (f32[2,1,1,32,256]{4,3,2,1,0:T(8,128)S(1)}, f32[2,1,1,32,256]{4,3,2,1,0:T(8,128)S(1)}, u32[]{:S(2)}, u32[]{:S(2)}) collective-permute-start(f32[2,1,1,32,256]{4,3,2,1,0:T(8,128)S(1)} %get-tuple-element.643), channel_id=1, source_target_pairs={{1,0},{2,1},{3,2},{4,3},{5,4},{6,5},{7,6},{9,8},{10,9},{11,10},{12... | collective-permute-start | bytes 196616 | tf_op jit(solution)/shard_map/while/body/eval_jaxpr/ppermute | solution.py:21
  131.8 8.0 %collective-permute-start.1 = (f32[2,1,1,32,256]{4,3,2,1,0:T(8,128)S(1)}, f32[2,1,1,32,256]{4,3,2,1,0:T(8,128)S(1)}, u32[]{:S(2)}, u32[]{:S(2)}) collective-permute-start(f32[2,1,1,32,256]{4,3,2,1,0:T(8,128)S(1)} %get-tuple-element.644), channel_id=1, source_target_pairs={{0,1},{1,2},{2,3},{3,4},{4,5},{5,6},{6,7},{8,9},{9,10},{10,11},{11... | collective-permute-start | bytes 196616 | tf_op jit(solution)/shard_map/while/body/eval_jaxpr/ppermute | solution.py:19
  149.7 7.3 %collective-permute-start.4 = (f32[1,1,32,256]{3,2,1,0:T(8,128)S(1)}, f32[1,1,32,256]{3,2,1,0:T(8,128)S(1)}, u32[]{:S(2)}, u32[]{:S(2)}) collective-permute-start(f32[1,1,32,256]{3,2,1,0:T(8,128)S(1)} %get-tuple-element.657), channel_id=1, source_target_pairs={{1,0},{2,1},{3,2},{4,3},{5,4},{6,5},{7,6},{9,8},{10,9},{11,10},{12... | collective-permute-start | bytes 98312 | tf_op jit(solution)/shard_map/while/body/eval_jaxpr/ppermute | solution.py:21
  151.0 7.6 %collective-permute-start.5 = (f32[1,1,32,256]{3,2,1,0:T(8,128)S(1)}, f32[1,1,32,256]{3,2,1,0:T(8,128)S(1)}, u32[]{:S(2)}, u32[]{:S(2)}) collective-permute-start(f32[1,1,32,256]{3,2,1,0:T(8,128)S(1)} %get-tuple-element.658), channel_id=1, source_target_pairs={{0,1},{1,2},{2,3},{3,4},{4,5},{5,6},{6,7},{8,9},{9,10},{10,11},{11... | collective-permute-start | bytes 98312 | tf_op jit(solution)/shard_map/while/body/eval_jaxpr/ppermute | solution.py:19
  160.8 12.0 %collective-permute-start.6 = (f32[2,1,1,32,256]{4,3,2,1,0:T(8,128)S(1)}, f32[2,1,1,32,256]{4,3,2,1,0:T(8,128)S(1)}, u32[]{:S(2)}, u32[]{:S(2)}) collective-permute-start(f32[2,1,1,32,256]{4,3,2,1,0:T(8,128)S(1)} %get-tuple-element.661), channel_id=1, source_target_pairs={{1,0},{2,1},{3,2},{4,3},{5,4},{6,5},{7,6},{9,8},{10,9},{11,10},{12... | collective-permute-start | bytes 196616 | tf_op jit(solution)/shard_map/while/body/eval_jaxpr/ppermute | solution.py:21
  162.2 10.5 %collective-permute-start.7 = (f32[2,1,1,32,256]{4,3,2,1,0:T(8,128)S(1)}, f32[2,1,1,32,256]{4,3,2,1,0:T(8,128)S(1)}, u32[]{:S(2)}, u32[]{:S(2)}) collective-permute-start(f32[2,1,1,32,256]{4,3,2,1,0:T(8,128)S(1)} %get-tuple-element.662), channel_id=1, source_target_pairs={{0,1},{1,2},{2,3},{3,4},{4,5},{5,6},{6,7},{8,9},{9,10},{10,11},{11... | collective-permute-start | bytes 196616 | tf_op jit(solution)/shard_map/while/body/eval_jaxpr/ppermute | solution.py:19
  173.9 7.4 %collective-permute-start = (f32[2,1,1,32,256]{4,3,2,1,0:T(8,128)S(1)}, f32[2,1,1,32,256]{4,3,2,1,0:T(8,128)S(1)}, u32[]{:S(2)}, u32[]{:S(2)}) collective-permute-start(f32[2,1,1,32,256]{4,3,2,1,0:T(8,128)S(1)} %get-tuple-element.643), channel_id=1, source_target_pairs={{1,0},{2,1},{3,2},{4,3},{5,4},{6,5},{7,6},{9,8},{10,9},{11,10},{12... | collective-permute-start | bytes 196616 | tf_op jit(solution)/shard_map/while/body/eval_jaxpr/ppermute | solution.py:21
  175.2 7.6 %collective-permute-start.1 = (f32[2,1,1,32,256]{4,3,2,1,0:T(8,128)S(1)}, f32[2,1,1,32,256]{4,3,2,1,0:T(8,128)S(1)}, u32[]{:S(2)}, u32[]{:S(2)}) collective-permute-start(f32[2,1,1,32,256]{4,3,2,1,0:T(8,128)S(1)} %get-tuple-element.644), channel_id=1, source_target_pairs={{0,1},{1,2},{2,3},{3,4},{4,5},{5,6},{6,7},{8,9},{9,10},{10,11},{11... | collective-permute-start | bytes 196616 | tf_op jit(solution)/shard_map/while/body/eval_jaxpr/ppermute | solution.py:19
  192.8 7.1 %collective-permute-start.4 = (f32[1,1,32,256]{3,2,1,0:T(8,128)S(1)}, f32[1,1,32,256]{3,2,1,0:T(8,128)S(1)}, u32[]{:S(2)}, u32[]{:S(2)}) collective-permute-start(f32[1,1,32,256]{3,2,1,0:T(8,128)S(1)} %get-tuple-element.657), channel_id=1, source_target_pairs={{1,0},{2,1},{3,2},{4,3},{5,4},{6,5},{7,6},{9,8},{10,9},{11,10},{12... | collective-permute-start | bytes 98312 | tf_op jit(solution)/shard_map/while/body/eval_jaxpr/ppermute | solution.py:21
  194.1 7.4 %collective-permute-start.5 = (f32[1,1,32,256]{3,2,1,0:T(8,128)S(1)}, f32[1,1,32,256]{3,2,1,0:T(8,128)S(1)}, u32[]{:S(2)}, u32[]{:S(2)}) collective-permute-start(f32[1,1,32,256]{3,2,1,0:T(8,128)S(1)} %get-tuple-element.658), channel_id=1, source_target_pairs={{0,1},{1,2},{2,3},{3,4},{4,5},{5,6},{6,7},{8,9},{9,10},{10,11},{11... | collective-permute-start | bytes 98312 | tf_op jit(solution)/shard_map/while/body/eval_jaxpr/ppermute | solution.py:19
  203.7 12.0 %collective-permute-start.6 = (f32[2,1,1,32,256]{4,3,2,1,0:T(8,128)S(1)}, f32[2,1,1,32,256]{4,3,2,1,0:T(8,128)S(1)}, u32[]{:S(2)}, u32[]{:S(2)}) collective-permute-start(f32[2,1,1,32,256]{4,3,2,1,0:T(8,128)S(1)} %get-tuple-element.661), channel_id=1, source_target_pairs={{1,0},{2,1},{3,2},{4,3},{5,4},{6,5},{7,6},{9,8},{10,9},{11,10},{12... | collective-permute-start | bytes 196616 | tf_op jit(solution)/shard_map/while/body/eval_jaxpr/ppermute | solution.py:21
  205.1 10.6 %collective-permute-start.7 = (f32[2,1,1,32,256]{4,3,2,1,0:T(8,128)S(1)}, f32[2,1,1,32,256]{4,3,2,1,0:T(8,128)S(1)}, u32[]{:S(2)}, u32[]{:S(2)}) collective-permute-start(f32[2,1,1,32,256]{4,3,2,1,0:T(8,128)S(1)} %get-tuple-element.662), channel_id=1, source_target_pairs={{0,1},{1,2},{2,3},{3,4},{4,5},{5,6},{6,7},{8,9},{9,10},{10,11},{11... | collective-permute-start | bytes 196616 | tf_op jit(solution)/shard_map/while/body/eval_jaxpr/ppermute | solution.py:19
  229.0 50.5 %all-to-all-start.2 = ((f32[4,1,4,32,256]{4,3,2,1,0:T(8,128)}), f32[4,1,4,32,256]{4,3,2,1,0:T(8,128)S(1)}, u32[]{:S(2)}, u32[]{:S(2)}) async-start(f32[4,1,4,32,256]{4,3,2,1,0:T(8,128)} %get-tuple-element.381), calls=%async_computation.2 | async-start | bytes 1048576 | tf_op jit(solution)/shard_map/all_to_all | solution.py:190
  (32 other events, 182.1 us)
where the time goes:
time: 283 us; the launch traced here: 281 us
  starting transfers between devices  119 us (42%)
  blocking collectives  79.4 us (28%)
  other arithmetic  33.1 us (12%)
  waiting for transfers between devices  20.6 us (7%)
  matrix products  17.5 us (6%)
  local copies, waits for them, and re-layouts  7.58 us (3%)
  loops' own time  3.42 us (1%)
    ppermute x16, starting transfers between devices, padded(): lax.ppermute(tail, axis, [(i, (i + 1) % count) for i in range(ends)])  89.6 us
    psum x1, blocking collectives, body(): totals = lax.psum(misfit, ('tm', 'space'))  46.4 us
    ppermute x16, starting transfers between devices, padded(): lax.ppermute(head, axis, [((i + 1) % count, i) for i in range(ends)])  21.2 us
    ppermute x16, waiting for transfers between devices, padded(): lax.ppermute(tail, axis, [(i, (i + 1) % count) for i in range(ends)])  18.9 us
    dot_general x4, matrix products, mismatch(): jnp.dot(pressure.reshape(batch_size, -1), well_picks.T, precision=lax.Pre...  16.2 us
    all_to_all x1, blocking collectives, body(): lax.all_to_all(result[2], 'tm', split_axis=0, concat_axis=1, tiled=True)  12.3 us
    add x2, other arithmetic, region_fields(): summed + jnp.where(region_ids == region_index, region_table[table_row, re...  10.3 us
    all_gather x1, blocking collectives, body(): lax.all_gather(inflow, 'tm', axis=0, tiled=True)  8.19 us
  transfers between devices with their start and end apart: 34, of which 17 were waited for; matrix products, arithmetic and copies ran while one was open for 13% of the time, Pallas kernels for 0%

commit v1 on v0

--- a/solution.py
+++ b/solution.py
@@ -190,7 +190,7 @@
         lax.all_to_all(result[3], "tm", split_axis=0, concat_axis=1, tiled=True),
     )
     misfit = lax.dynamic_update_slice_in_dim(misfit, result[4], section_index * batch_size, 0)
-    totals = lax.psum(misfit, ("tm", "space"))
+    totals = jnp.sum(lax.all_gather(misfit, ("tm", "space")), axis=0)
     return (totals / (sections * REP_DEV * well_cells.shape[0]), slab_pressure, slab_saturation)
 
 

time: 283 us -> 308 us (1.088)
  blocking collectives: 79.4 us -> 104 us
    all_gather x0 -> x1, blocking collectives: none -> 71.4 us  [body(): totals = jnp.sum(lax.all_gather(misfit, ('tm', 'space')), axis=0)]
    psum x1 -> x0, blocking collectives: 46.4 us -> none  [body(): totals = lax.psum(misfit, ('tm', 'space'))]
  transfers between devices with their start and end apart: 34 -> 34, of which waited for: 17 -> 17; matrix products, arithmetic and copies ran while one was open for 13% -> 12% of each run, Pallas kernels for 0% -> 0%
where the time goes in v1:
time: 308 us; the launch traced here: 306 us
  starting transfers between devices  119 us (39%)
  blocking collectives  104 us (34%)
  other arithmetic  33.2 us (11%)
  waiting for transfers between devices  20.6 us (7%)
  matrix products  17.5 us (6%)
  local copies, waits for them, and re-layouts  7.51 us (2%)
  loops' own time  3.42 us (1%)
    ppermute x16, starting transfers between devices, padded(): lax.ppermute(tail, axis, [(i, (i + 1) % count) for i in range(ends)])  89.6 us
    all_gather x1, blocking collectives, body(): totals = jnp.sum(lax.all_gather(misfit, ('tm', 'space')), axis=0)  71.4 us
    ppermute x16, starting transfers between devices, padded(): lax.ppermute(head, axis, [((i + 1) % count, i) for i in range(ends)])  21.2 us
    ppermute x16, waiting for transfers between devices, padded(): lax.ppermute(tail, axis, [(i, (i + 1) % count) for i in range(ends)])  18.9 us
    dot_general x4, matrix products, mismatch(): jnp.dot(pressure.reshape(batch_size, -1), well_picks.T, precision=lax.Pre...  16.2 us
    all_to_all x1, blocking collectives, body(): lax.all_to_all(result[2], 'tm', split_axis=0, concat_axis=1, tiled=True)  12.3 us
    add x2, other arithmetic, region_fields(): summed + jnp.where(region_ids == region_index, region_table[table_row, re...  10.3 us
    all_gather x1, blocking collectives, body(): lax.all_gather(inflow, 'tm', axis=0, tiled=True)  8.19 us
  transfers between devices with their start and end apart: 34, of which 17 were waited for; matrix products, arithmetic and copies ran while one was open for 12% of the time, Pallas kernels for 0%

profile of v1, /device:TPU:0, one launch (start us, length us, event | category | flops | bytes accessed | tf_op | source)
XLA Modules:
  0.0 306.1 jit_solution(3747747486979522698)
XLA Ops:
  6.7 5.2 %all-gather = f32[4,1,32]{2,1,0:T(1,128)S(1)} all-gather(f32[1,1,32]{2,1,0:T(1,128)S(1)} %bitcast.155), channel_id=1, replica_groups=mesh['tm'=4,'space'=8] {'tm'}, dimensions={0}, use_global_device_ids=true | all-gather | bytes 640 | tf_op jit(solution)/shard_map/all_gather | solution.py:157
  13.9 8.2 %all_gather.19 = f32[4,4,32,256]{3,2,1,0:T(8,128)} all-gather(f32[1,4,32,256]{3,2,1,0:T(8,128)S(1)} %copy-done.7), channel_id=1, replica_groups=mesh['tm'=4,'space'=8] {'tm'}, dimensions={0}, use_global_device_ids=true | all-gather | bytes 655360 | tf_op jit(solution)/shard_map/all_gather | solution.py:156
  22.1 7.4 %all_gather.20 = f32[4,4,32,256]{3,2,1,0:T(8,128)S(1)} all-gather(f32[1,4,32,256]{3,2,1,0:T(8,128)S(1)} %copy-done.8), channel_id=1, replica_groups=mesh['tm'=4,'space'=8] {'tm'}, dimensions={0}, use_global_device_ids=true | all-gather | bytes 655360 | tf_op jit(solution)/shard_map/all_gather | solution.py:155
  29.6 5.2 %select_add_fusion = (f32[4,32,256]{2,1,0:T(8,128)S(1)}, pred[4,32,256]{2,1,0:T(8,128)(4,1)S(1)}, pred[4,32,256]{2,1,0:T(8,128)(4,1)S(1)}, pred[4,32,256]{2,1,0:...) fusion(f32[]{:T(128)} %bitcast.28, f32[]{:T(128)} %bitcast.27, ...), kind=kLoop, calls=%fused_computation.152 | loop fusion | flops 753664 | bytes 524320 | tf_op jit(solution)/shard_map/add | solution.py:96
  34.8 5.1 %add_multiply_fusion = f32[4,32,256]{2,1,0:T(8,128)S(1)} fusion(pred[4,32,256]{2,1,0:T(8,128)(4,1)S(1)} %get-tuple-element.474, pred[4,32,256]{2,1,0:T(8,128)(4,1)S(1)} %get-tuple-element.473, pred[4,32,256]{2,1,0:T(8,128)(4,1)S(1)} %get-tuple-element.472, pred[4,32,256]{2,1,0:T(8,128)(4,1)S(1)} %get-tuple-element.471, ...), kind=kLoop, calls=%fused_computation.153 | loop fusion | flops 524288 | bytes 393248 | tf_op jit(solution)/shard_map/mul | solution.py:100
  39.8 5.1 %select_add_fusion.1 = f32[4,32,256]{2,1,0:T(8,128)S(1)} fusion(pred[4,32,256]{2,1,0:T(8,128)(4,1)S(1)} %get-tuple-element.474, pred[4,32,256]{2,1,0:T(8,128)(4,1)S(1)} %get-tuple-element.473, pred[4,32,256]{2,1,0:T(8,128)(4,1)S(1)} %get-tuple-element.472, pred[4,32,256]{2,1,0:T(8,128)(4,1)S(1)} %get-tuple-element.471, ...), kind=kLoop, calls=%fused_computation.155 | loop fusion | flops 491520 | bytes 393248 | tf_op jit(solution)/shard_map/add | solution.py:96
  46.0 170.8 %while.24 = (s32[]{:T(128)}, f32[1,4,32,256]{3,2,1,0:T(8,128)S(1)}, f32[1,4,32,256]{3,2,1,0:T(8,128)S(1)}, f32[4,1,4,32,256]{4,3,2,1,0:T(8,128)}, f32[4,1,4,32,2...) while((s32[]{:T(128)}, f32[1,4,32,256]{3,2,1,0:T(8,128)S(1)}, ...), condition=%wide.region_3.4_spmd.clone, body=%wide.region_1.3_spmd.clone.sunk | while | flops 19529856 | bytes 16516069 | solution.py:182
  56.7 5.1 %collective-permute-start.3 = (f32[1,1,32,256]{3,2,1,0:T(8,128)S(1)}, f32[1,1,32,256]{3,2,1,0:T(8,128)S(1)}, u32[]{:S(2)}, u32[]{:S(2)}) collective-permute-start(f32[1,1,32,256]{3,2,1,0:T(8,128)S(1)} %get-tuple-element.656), channel_id=1, source_target_pairs={{0,1},{1,2},{2,3},{3,4},{4,5},{5,6},{6,7},{8,9},{9,10},{10,11},{11... | collective-permute-start | bytes 98312 | tf_op jit(solution)/shard_map/while/body/eval_jaxpr/ppermute | solution.py:19
  64.9 5.8 %collective-permute-start.5 = (f32[1,1,32,256]{3,2,1,0:T(8,128)S(1)}, f32[1,1,32,256]{3,2,1,0:T(8,128)S(1)}, u32[]{:S(2)}, u32[]{:S(2)}) collective-permute-start(f32[1,1,32,256]{3,2,1,0:T(8,128)S(1)} %get-tuple-element.658), channel_id=1, source_target_pairs={{0,1},{1,2},{2,3},{3,4},{4,5},{5,6},{6,7},{8,9},{9,10},{10,11},{11... | collective-permute-start | bytes 98312 | tf_op jit(solution)/shard_map/while/body/eval_jaxpr/ppermute | solution.py:19
  75.9 5.8 %collective-permute-start.7 = (f32[2,1,1,32,256]{4,3,2,1,0:T(8,128)S(1)}, f32[2,1,1,32,256]{4,3,2,1,0:T(8,128)S(1)}, u32[]{:S(2)}, u32[]{:S(2)}) collective-permute-start(f32[2,1,1,32,256]{4,3,2,1,0:T(8,128)S(1)} %get-tuple-element.662), channel_id=1, source_target_pairs={{0,1},{1,2},{2,3},{3,4},{4,5},{5,6},{6,7},{8,9},{9,10},{10,11},{11... | collective-permute-start | bytes 196616 | tf_op jit(solution)/shard_map/while/body/eval_jaxpr/ppermute | solution.py:19
  88.9 5.8 %collective-permute-start.1 = (f32[2,1,1,32,256]{4,3,2,1,0:T(8,128)S(1)}, f32[2,1,1,32,256]{4,3,2,1,0:T(8,128)S(1)}, u32[]{:S(2)}, u32[]{:S(2)}) collective-permute-start(f32[2,1,1,32,256]{4,3,2,1,0:T(8,128)S(1)} %get-tuple-element.644), channel_id=1, source_target_pairs={{0,1},{1,2},{2,3},{3,4},{4,5},{5,6},{6,7},{8,9},{9,10},{10,11},{11... | collective-permute-start | bytes 196616 | tf_op jit(solution)/shard_map/while/body/eval_jaxpr/ppermute | solution.py:19
  99.3 5.4 %collective-permute-start.3 = (f32[1,1,32,256]{3,2,1,0:T(8,128)S(1)}, f32[1,1,32,256]{3,2,1,0:T(8,128)S(1)}, u32[]{:S(2)}, u32[]{:S(2)}) collective-permute-start(f32[1,1,32,256]{3,2,1,0:T(8,128)S(1)} %get-tuple-element.656), channel_id=1, source_target_pairs={{0,1},{1,2},{2,3},{3,4},{4,5},{5,6},{6,7},{8,9},{9,10},{10,11},{11... | collective-permute-start | bytes 98312 | tf_op jit(solution)/shard_map/while/body/eval_jaxpr/ppermute | solution.py:19
  107.8 5.8 %collective-permute-start.5 = (f32[1,1,32,256]{3,2,1,0:T(8,128)S(1)}, f32[1,1,32,256]{3,2,1,0:T(8,128)S(1)}, u32[]{:S(2)}, u32[]{:S(2)}) collective-permute-start(f32[1,1,32,256]{3,2,1,0:T(8,128)S(1)} %get-tuple-element.658), channel_id=1, source_target_pairs={{0,1},{1,2},{2,3},{3,4},{4,5},{5,6},{6,7},{8,9},{9,10},{10,11},{11... | collective-permute-start | bytes 98312 | tf_op jit(solution)/shard_map/while/body/eval_jaxpr/ppermute | solution.py:19
  118.8 5.8 %collective-permute-start.7 = (f32[2,1,1,32,256]{4,3,2,1,0:T(8,128)S(1)}, f32[2,1,1,32,256]{4,3,2,1,0:T(8,128)S(1)}, u32[]{:S(2)}, u32[]{:S(2)}) collective-permute-start(f32[2,1,1,32,256]{4,3,2,1,0:T(8,128)S(1)} %get-tuple-element.662), channel_id=1, source_target_pairs={{0,1},{1,2},{2,3},{3,4},{4,5},{5,6},{6,7},{8,9},{9,10},{10,11},{11... | collective-permute-start | bytes 196616 | tf_op jit(solution)/shard_map/while/body/eval_jaxpr/ppermute | solution.py:19
  131.8 5.9 %collective-permute-start.1 = (f32[2,1,1,32,256]{4,3,2,1,0:T(8,128)S(1)}, f32[2,1,1,32,256]{4,3,2,1,0:T(8,128)S(1)}, u32[]{:S(2)}, u32[]{:S(2)}) collective-permute-start(f32[2,1,1,32,256]{4,3,2,1,0:T(8,128)S(1)} %get-tuple-element.644), channel_id=1, source_target_pairs={{0,1},{1,2},{2,3},{3,4},{4,5},{5,6},{6,7},{8,9},{9,10},{10,11},{11... | collective-permute-start | bytes 196616 | tf_op jit(solution)/shard_map/while/body/eval_jaxpr/ppermute | solution.py:19
  142.6 5.4 %collective-permute-start.3 = (f32[1,1,32,256]{3,2,1,0:T(8,128)S(1)}, f32[1,1,32,256]{3,2,1,0:T(8,128)S(1)}, u32[]{:S(2)}, u32[]{:S(2)}) collective-permute-start(f32[1,1,32,256]{3,2,1,0:T(8,128)S(1)} %get-tuple-element.656), channel_id=1, source_target_pairs={{0,1},{1,2},{2,3},{3,4},{4,5},{5,6},{6,7},{8,9},{9,10},{10,11},{11... | collective-permute-start | bytes 98312 | tf_op jit(solution)/shard_map/while/body/eval_jaxpr/ppermute | solution.py:19
  151.0 5.9 %collective-permute-start.5 = (f32[1,1,32,256]{3,2,1,0:T(8,128)S(1)}, f32[1,1,32,256]{3,2,1,0:T(8,128)S(1)}, u32[]{:S(2)}, u32[]{:S(2)}) collective-permute-start(f32[1,1,32,256]{3,2,1,0:T(8,128)S(1)} %get-tuple-element.658), channel_id=1, source_target_pairs={{0,1},{1,2},{2,3},{3,4},{4,5},{5,6},{6,7},{8,9},{9,10},{10,11},{11... | collective-permute-start | bytes 98312 | tf_op jit(solution)/shard_map/while/body/eval_jaxpr/ppermute | solution.py:19
  162.2 5.7 %collective-permute-start.7 = (f32[2,1,1,32,256]{4,3,2,1,0:T(8,128)S(1)}, f32[2,1,1,32,256]{4,3,2,1,0:T(8,128)S(1)}, u32[]{:S(2)}, u32[]{:S(2)}) collective-permute-start(f32[2,1,1,32,256]{4,3,2,1,0:T(8,128)S(1)} %get-tuple-element.662), channel_id=1, source_target_pairs={{0,1},{1,2},{2,3},{3,4},{4,5},{5,6},{6,7},{8,9},{9,10},{10,11},{11... | collective-permute-start | bytes 196616 | tf_op jit(solution)/shard_map/while/body/eval_jaxpr/ppermute | solution.py:19
  175.2 5.8 %collective-permute-start.1 = (f32[2,1,1,32,256]{4,3,2,1,0:T(8,128)S(1)}, f32[2,1,1,32,256]{4,3,2,1,0:T(8,128)S(1)}, u32[]{:S(2)}, u32[]{:S(2)}) collective-permute-start(f32[2,1,1,32,256]{4,3,2,1,0:T(8,128)S(1)} %get-tuple-element.644), channel_id=1, source_target_pairs={{0,1},{1,2},{2,3},{3,4},{4,5},{5,6},{6,7},{8,9},{9,10},{10,11},{11... | collective-permute-start | bytes 196616 | tf_op jit(solution)/shard_map/while/body/eval_jaxpr/ppermute | solution.py:19
  185.6 5.4 %collective-permute-start.3 = (f32[1,1,32,256]{3,2,1,0:T(8,128)S(1)}, f32[1,1,32,256]{3,2,1,0:T(8,128)S(1)}, u32[]{:S(2)}, u32[]{:S(2)}) collective-permute-start(f32[1,1,32,256]{3,2,1,0:T(8,128)S(1)} %get-tuple-element.656), channel_id=1, source_target_pairs={{0,1},{1,2},{2,3},{3,4},{4,5},{5,6},{6,7},{8,9},{9,10},{10,11},{11... | collective-permute-start | bytes 98312 | tf_op jit(solution)/shard_map/while/body/eval_jaxpr/ppermute | solution.py:19
  194.1 5.8 %collective-permute-start.5 = (f32[1,1,32,256]{3,2,1,0:T(8,128)S(1)}, f32[1,1,32,256]{3,2,1,0:T(8,128)S(1)}, u32[]{:S(2)}, u32[]{:S(2)}) collective-permute-start(f32[1,1,32,256]{3,2,1,0:T(8,128)S(1)} %get-tuple-element.658), channel_id=1, source_target_pairs={{0,1},{1,2},{2,3},{3,4},{4,5},{5,6},{6,7},{8,9},{9,10},{10,11},{11... | collective-permute-start | bytes 98312 | tf_op jit(solution)/shard_map/while/body/eval_jaxpr/ppermute | solution.py:19
  205.1 5.8 %collective-permute-start.7 = (f32[2,1,1,32,256]{4,3,2,1,0:T(8,128)S(1)}, f32[2,1,1,32,256]{4,3,2,1,0:T(8,128)S(1)}, u32[]{:S(2)}, u32[]{:S(2)}) collective-permute-start(f32[2,1,1,32,256]{4,3,2,1,0:T(8,128)S(1)} %get-tuple-element.662), channel_id=1, source_target_pairs={{0,1},{1,2},{2,3},{3,4},{4,5},{5,6},{6,7},{8,9},{9,10},{10,11},{11... | collective-permute-start | bytes 196616 | tf_op jit(solution)/shard_map/while/body/eval_jaxpr/ppermute | solution.py:19
  216.8 12.3 %all_to_all.36 = f32[4,1,4,32,256]{4,3,2,1,0:T(8,128)S(1)} all-to-all(f32[4,1,4,32,256]{4,3,2,1,0:T(8,128)} %get-tuple-element.380), channel_id=1, replica_groups=mesh['tm'=4,'space'=8] {'tm'}, dimensions={0} | all-to-all | bytes 1048576 | tf_op jit(solution)/shard_map/all_to_all | solution.py:189
  232.6 71.4 %all-gather.1 = f32[32,1,4]{2,1,0:T(1,128)S(1)} all-gather(f32[1,1,4]{2,1,0:T(1,128)S(1)} %dynamic_update_slice.26), channel_id=1, replica_groups=mesh['tm'=4,'space'=8] {'tm','space'}, dimensions={0}, use_global_device_ids=true | all-gather | bytes 528 | tf_op jit(solution)/shard_map/all_gather | solution.py:193
  (190 shorter events, 97.1 us)
Async XLA Ops:
  0.7 44.4 %all-to-all-start = ((f32[4,1,32]{2,1,0:T(1,128)}), f32[4,1,32]{2,1,0:T(1,128)S(1)}, u32[]{:S(2)}, u32[]{:S(2)}) async-start(f32[4,1,32]{2,1,0:T(1,128)} %param.21), calls=%async_computation | async-start | bytes 4096 | tf_op jit(solution)/shard_map/all_to_all | solution.py:159
  63.6 7.1 %collective-permute-start.4 = (f32[1,1,32,256]{3,2,1,0:T(8,128)S(1)}, f32[1,1,32,256]{3,2,1,0:T(8,128)S(1)}, u32[]{:S(2)}, u32[]{:S(2)}) collective-permute-start(f32[1,1,32,256]{3,2,1,0:T(8,128)S(1)} %get-tuple-element.657), channel_id=1, source_target_pairs={{1,0},{2,1},{3,2},{4,3},{5,4},{6,5},{7,6},{9,8},{10,9},{11,10},{12... | collective-permute-start | bytes 98312 | tf_op jit(solution)/shard_map/while/body/eval_jaxpr/ppermute | solution.py:21
  64.9 7.4 %collective-permute-start.5 = (f32[1,1,32,256]{3,2,1,0:T(8,128)S(1)}, f32[1,1,32,256]{3,2,1,0:T(8,128)S(1)}, u32[]{:S(2)}, u32[]{:S(2)}) collective-permute-start(f32[1,1,32,256]{3,2,1,0:T(8,128)S(1)} %get-tuple-element.658), channel_id=1, source_target_pairs={{0,1},{1,2},{2,3},{3,4},{4,5},{5,6},{6,7},{8,9},{9,10},{10,11},{11... | collective-permute-start | bytes 98312 | tf_op jit(solution)/shard_map/while/body/eval_jaxpr/ppermute | solution.py:19
  74.4 12.0 %collective-permute-start.6 = (f32[2,1,1,32,256]{4,3,2,1,0:T(8,128)S(1)}, f32[2,1,1,32,256]{4,3,2,1,0:T(8,128)S(1)}, u32[]{:S(2)}, u32[]{:S(2)}) collective-permute-start(f32[2,1,1,32,256]{4,3,2,1,0:T(8,128)S(1)} %get-tuple-element.661), channel_id=1, source_target_pairs={{1,0},{2,1},{3,2},{4,3},{5,4},{6,5},{7,6},{9,8},{10,9},{11,10},{12... | collective-permute-start | bytes 196616 | tf_op jit(solution)/shard_map/while/body/eval_jaxpr/ppermute | solution.py:21
  75.9 10.6 %collective-permute-start.7 = (f32[2,1,1,32,256]{4,3,2,1,0:T(8,128)S(1)}, f32[2,1,1,32,256]{4,3,2,1,0:T(8,128)S(1)}, u32[]{:S(2)}, u32[]{:S(2)}) collective-permute-start(f32[2,1,1,32,256]{4,3,2,1,0:T(8,128)S(1)} %get-tuple-element.662), channel_id=1, source_target_pairs={{0,1},{1,2},{2,3},{3,4},{4,5},{5,6},{6,7},{8,9},{9,10},{10,11},{11... | collective-permute-start | bytes 196616 | tf_op jit(solution)/shard_map/while/body/eval_jaxpr/ppermute | solution.py:19
  87.6 7.4 %collective-permute-start = (f32[2,1,1,32,256]{4,3,2,1,0:T(8,128)S(1)}, f32[2,1,1,32,256]{4,3,2,1,0:T(8,128)S(1)}, u32[]{:S(2)}, u32[]{:S(2)}) collective-permute-start(f32[2,1,1,32,256]{4,3,2,1,0:T(8,128)S(1)} %get-tuple-element.643), channel_id=1, source_target_pairs={{1,0},{2,1},{3,2},{4,3},{5,4},{6,5},{7,6},{9,8},{10,9},{11,10},{12... | collective-permute-start | bytes 196616 | tf_op jit(solution)/shard_map/while/body/eval_jaxpr/ppermute | solution.py:21
  88.9 7.6 %collective-permute-start.1 = (f32[2,1,1,32,256]{4,3,2,1,0:T(8,128)S(1)}, f32[2,1,1,32,256]{4,3,2,1,0:T(8,128)S(1)}, u32[]{:S(2)}, u32[]{:S(2)}) collective-permute-start(f32[2,1,1,32,256]{4,3,2,1,0:T(8,128)S(1)} %get-tuple-element.644), channel_id=1, source_target_pairs={{0,1},{1,2},{2,3},{3,4},{4,5},{5,6},{6,7},{8,9},{9,10},{10,11},{11... | collective-permute-start | bytes 196616 | tf_op jit(solution)/shard_map/while/body/eval_jaxpr/ppermute | solution.py:19
  106.5 7.1 %collective-permute-start.4 = (f32[1,1,32,256]{3,2,1,0:T(8,128)S(1)}, f32[1,1,32,256]{3,2,1,0:T(8,128)S(1)}, u32[]{:S(2)}, u32[]{:S(2)}) collective-permute-start(f32[1,1,32,256]{3,2,1,0:T(8,128)S(1)} %get-tuple-element.657), channel_id=1, source_target_pairs={{1,0},{2,1},{3,2},{4,3},{5,4},{6,5},{7,6},{9,8},{10,9},{11,10},{12... | collective-permute-start | bytes 98312 | tf_op jit(solution)/shard_map/while/body/eval_jaxpr/ppermute | solution.py:21
  107.8 7.4 %collective-permute-start.5 = (f32[1,1,32,256]{3,2,1,0:T(8,128)S(1)}, f32[1,1,32,256]{3,2,1,0:T(8,128)S(1)}, u32[]{:S(2)}, u32[]{:S(2)}) collective-permute-start(f32[1,1,32,256]{3,2,1,0:T(8,128)S(1)} %get-tuple-element.658), channel_id=1, source_target_pairs={{0,1},{1,2},{2,3},{3,4},{4,5},{5,6},{6,7},{8,9},{9,10},{10,11},{11... | collective-permute-start | bytes 98312 | tf_op jit(solution)/shard_map/while/body/eval_jaxpr/ppermute | solution.py:19
  117.4 12.0 %collective-permute-start.6 = (f32[2,1,1,32,256]{4,3,2,1,0:T(8,128)S(1)}, f32[2,1,1,32,256]{4,3,2,1,0:T(8,128)S(1)}, u32[]{:S(2)}, u32[]{:S(2)}) collective-permute-start(f32[2,1,1,32,256]{4,3,2,1,0:T(8,128)S(1)} %get-tuple-element.661), channel_id=1, source_target_pairs={{1,0},{2,1},{3,2},{4,3},{5,4},{6,5},{7,6},{9,8},{10,9},{11,10},{12... | collective-permute-start | bytes 196616 | tf_op jit(solution)/shard_map/while/body/eval_jaxpr/ppermute | solution.py:21
  118.8 10.6 %collective-permute-start.7 = (f32[2,1,1,32,256]{4,3,2,1,0:T(8,128)S(1)}, f32[2,1,1,32,256]{4,3,2,1,0:T(8,128)S(1)}, u32[]{:S(2)}, u32[]{:S(2)}) collective-permute-start(f32[2,1,1,32,256]{4,3,2,1,0:T(8,128)S(1)} %get-tuple-element.662), channel_id=1, source_target_pairs={{0,1},{1,2},{2,3},{3,4},{4,5},{5,6},{6,7},{8,9},{9,10},{10,11},{11... | collective-permute-start | bytes 196616 | tf_op jit(solution)/shard_map/while/body/eval_jaxpr/ppermute | solution.py:19
  130.5 7.6 %collective-permute-start = (f32[2,1,1,32,256]{4,3,2,1,0:T(8,128)S(1)}, f32[2,1,1,32,256]{4,3,2,1,0:T(8,128)S(1)}, u32[]{:S(2)}, u32[]{:S(2)}) collective-permute-start(f32[2,1,1,32,256]{4,3,2,1,0:T(8,128)S(1)} %get-tuple-element.643), channel_id=1, source_target_pairs={{1,0},{2,1},{3,2},{4,3},{5,4},{6,5},{7,6},{9,8},{10,9},{11,10},{12... | collective-permute-start | bytes 196616 | tf_op jit(solution)/shard_map/while/body/eval_jaxpr/ppermute | solution.py:21
  131.8 8.0 %collective-permute-start.1 = (f32[2,1,1,32,256]{4,3,2,1,0:T(8,128)S(1)}, f32[2,1,1,32,256]{4,3,2,1,0:T(8,128)S(1)}, u32[]{:S(2)}, u32[]{:S(2)}) collective-permute-start(f32[2,1,1,32,256]{4,3,2,1,0:T(8,128)S(1)} %get-tuple-element.644), channel_id=1, source_target_pairs={{0,1},{1,2},{2,3},{3,4},{4,5},{5,6},{6,7},{8,9},{9,10},{10,11},{11... | collective-permute-start | bytes 196616 | tf_op jit(solution)/shard_map/while/body/eval_jaxpr/ppermute | solution.py:19
  149.7 7.3 %collective-permute-start.4 = (f32[1,1,32,256]{3,2,1,0:T(8,128)S(1)}, f32[1,1,32,256]{3,2,1,0:T(8,128)S(1)}, u32[]{:S(2)}, u32[]{:S(2)}) collective-permute-start(f32[1,1,32,256]{3,2,1,0:T(8,128)S(1)} %get-tuple-element.657), channel_id=1, source_target_pairs={{1,0},{2,1},{3,2},{4,3},{5,4},{6,5},{7,6},{9,8},{10,9},{11,10},{12... | collective-permute-start | bytes 98312 | tf_op jit(solution)/shard_map/while/body/eval_jaxpr/ppermute | solution.py:21
  151.0 7.6 %collective-permute-start.5 = (f32[1,1,32,256]{3,2,1,0:T(8,128)S(1)}, f32[1,1,32,256]{3,2,1,0:T(8,128)S(1)}, u32[]{:S(2)}, u32[]{:S(2)}) collective-permute-start(f32[1,1,32,256]{3,2,1,0:T(8,128)S(1)} %get-tuple-element.658), channel_id=1, source_target_pairs={{0,1},{1,2},{2,3},{3,4},{4,5},{5,6},{6,7},{8,9},{9,10},{10,11},{11... | collective-permute-start | bytes 98312 | tf_op jit(solution)/shard_map/while/body/eval_jaxpr/ppermute | solution.py:19
  160.8 12.0 %collective-permute-start.6 = (f32[2,1,1,32,256]{4,3,2,1,0:T(8,128)S(1)}, f32[2,1,1,32,256]{4,3,2,1,0:T(8,128)S(1)}, u32[]{:S(2)}, u32[]{:S(2)}) collective-permute-start(f32[2,1,1,32,256]{4,3,2,1,0:T(8,128)S(1)} %get-tuple-element.661), channel_id=1, source_target_pairs={{1,0},{2,1},{3,2},{4,3},{5,4},{6,5},{7,6},{9,8},{10,9},{11,10},{12... | collective-permute-start | bytes 196616 | tf_op jit(solution)/shard_map/while/body/eval_jaxpr/ppermute | solution.py:21
  162.2 10.5 %collective-permute-start.7 = (f32[2,1,1,32,256]{4,3,2,1,0:T(8,128)S(1)}, f32[2,1,1,32,256]{4,3,2,1,0:T(8,128)S(1)}, u32[]{:S(2)}, u32[]{:S(2)}) collective-permute-start(f32[2,1,1,32,256]{4,3,2,1,0:T(8,128)S(1)} %get-tuple-element.662), channel_id=1, source_target_pairs={{0,1},{1,2},{2,3},{3,4},{4,5},{5,6},{6,7},{8,9},{9,10},{10,11},{11... | collective-permute-start | bytes 196616 | tf_op jit(solution)/shard_map/while/body/eval_jaxpr/ppermute | solution.py:19
  173.9 7.4 %collective-permute-start = (f32[2,1,1,32,256]{4,3,2,1,0:T(8,128)S(1)}, f32[2,1,1,32,256]{4,3,2,1,0:T(8,128)S(1)}, u32[]{:S(2)}, u32[]{:S(2)}) collective-permute-start(f32[2,1,1,32,256]{4,3,2,1,0:T(8,128)S(1)} %get-tuple-element.643), channel_id=1, source_target_pairs={{1,0},{2,1},{3,2},{4,3},{5,4},{6,5},{7,6},{9,8},{10,9},{11,10},{12... | collective-permute-start | bytes 196616 | tf_op jit(solution)/shard_map/while/body/eval_jaxpr/ppermute | solution.py:21
  175.2 7.6 %collective-permute-start.1 = (f32[2,1,1,32,256]{4,3,2,1,0:T(8,128)S(1)}, f32[2,1,1,32,256]{4,3,2,1,0:T(8,128)S(1)}, u32[]{:S(2)}, u32[]{:S(2)}) collective-permute-start(f32[2,1,1,32,256]{4,3,2,1,0:T(8,128)S(1)} %get-tuple-element.644), channel_id=1, source_target_pairs={{0,1},{1,2},{2,3},{3,4},{4,5},{5,6},{6,7},{8,9},{9,10},{10,11},{11... | collective-permute-start | bytes 196616 | tf_op jit(solution)/shard_map/while/body/eval_jaxpr/ppermute | solution.py:19
  192.8 7.1 %collective-permute-start.4 = (f32[1,1,32,256]{3,2,1,0:T(8,128)S(1)}, f32[1,1,32,256]{3,2,1,0:T(8,128)S(1)}, u32[]{:S(2)}, u32[]{:S(2)}) collective-permute-start(f32[1,1,32,256]{3,2,1,0:T(8,128)S(1)} %get-tuple-element.657), channel_id=1, source_target_pairs={{1,0},{2,1},{3,2},{4,3},{5,4},{6,5},{7,6},{9,8},{10,9},{11,10},{12... | collective-permute-start | bytes 98312 | tf_op jit(solution)/shard_map/while/body/eval_jaxpr/ppermute | solution.py:21
  194.1 7.4 %collective-permute-start.5 = (f32[1,1,32,256]{3,2,1,0:T(8,128)S(1)}, f32[1,1,32,256]{3,2,1,0:T(8,128)S(1)}, u32[]{:S(2)}, u32[]{:S(2)}) collective-permute-start(f32[1,1,32,256]{3,2,1,0:T(8,128)S(1)} %get-tuple-element.658), channel_id=1, source_target_pairs={{0,1},{1,2},{2,3},{3,4},{4,5},{5,6},{6,7},{8,9},{9,10},{10,11},{11... | collective-permute-start | bytes 98312 | tf_op jit(solution)/shard_map/while/body/eval_jaxpr/ppermute | solution.py:19
  203.7 12.0 %collective-permute-start.6 = (f32[2,1,1,32,256]{4,3,2,1,0:T(8,128)S(1)}, f32[2,1,1,32,256]{4,3,2,1,0:T(8,128)S(1)}, u32[]{:S(2)}, u32[]{:S(2)}) collective-permute-start(f32[2,1,1,32,256]{4,3,2,1,0:T(8,128)S(1)} %get-tuple-element.661), channel_id=1, source_target_pairs={{1,0},{2,1},{3,2},{4,3},{5,4},{6,5},{7,6},{9,8},{10,9},{11,10},{12... | collective-permute-start | bytes 196616 | tf_op jit(solution)/shard_map/while/body/eval_jaxpr/ppermute | solution.py:21
  205.1 10.6 %collective-permute-start.7 = (f32[2,1,1,32,256]{4,3,2,1,0:T(8,128)S(1)}, f32[2,1,1,32,256]{4,3,2,1,0:T(8,128)S(1)}, u32[]{:S(2)}, u32[]{:S(2)}) collective-permute-start(f32[2,1,1,32,256]{4,3,2,1,0:T(8,128)S(1)} %get-tuple-element.662), channel_id=1, source_target_pairs={{0,1},{1,2},{2,3},{3,4},{4,5},{5,6},{6,7},{8,9},{9,10},{10,11},{11... | collective-permute-start | bytes 196616 | tf_op jit(solution)/shard_map/while/body/eval_jaxpr/ppermute | solution.py:19
  229.0 75.5 %all-to-all-start.2 = ((f32[4,1,4,32,256]{4,3,2,1,0:T(8,128)}), f32[4,1,4,32,256]{4,3,2,1,0:T(8,128)S(1)}, u32[]{:S(2)}, u32[]{:S(2)}) async-start(f32[4,1,4,32,256]{4,3,2,1,0:T(8,128)} %get-tuple-element.381), calls=%async_computation.2 | async-start | bytes 1048576 | tf_op jit(solution)/shard_map/all_to_all | solution.py:190
  (32 other events, 182.1 us)
